TPU v7x, 512 devices: a whole 4x8x8 slice. The times are simulated.
512 devices in a mesh: sector: 32 (over z_lo, x, core), term: 16 (over z_hi, y).
Axes of the slice: x: 4, y: 8, z: 8 (z_hi: 2, z_lo: 4; z = z_hi * 4 + z_lo), core: 2. Of those that a mesh axis runs over, the one named last changes fastest.
Arguments:
- wave: float32 [32, 512, 512], P('sector', 'term'), may hold values from -12 to 12
- left_ops: bfloat16 [64, 32, 512, 512], P('term', 'sector'), may hold values from -4 to 4
- right_ops: bfloat16 [64, 32, 512, 512], P('term', 'sector'), may hold values from -4 to 4
- charges: int32 [64], replicated, may hold values from -1 to 1, as said below
- diag: float32 [32, 512, 512], P('sector', 'term'), may hold values from 0.5 to 8
Outputs:
- psi_out: float32 [32, 512, 512], P('sector', 'term')
Inputs may be any that keep to these rules, and one draw needn't show every extreme that they name: `charges`: exactly (65) // 2 terms have charge 0; at least one term has charge 1 and at least one has charge -1.
All inputs are finite; a program needn't handle non-finite values.
Results may differ from a plain program's by a relative error of at most 0.0085.
Values may be sent and summed in bfloat16 or wider, within the bound.
A program may use at most 64 MiB of HBM per device.

v0:
```python
import jax
import jax.numpy as jnp
from jax import lax
from jax.sharding import PartitionSpec as P

STEPS = 3


def sent_together(arrays, axis, dim, along):
    both = jnp.concatenate(arrays, axis=along)
    result, at, done = (lax.all_gather(both, axis, axis=dim, tiled=True), 0, [])
    for a in arrays:
        done.append(lax.slice_in_dim(result, at, at + a.shape[along], axis=along))
        at += a.shape[along]
    return tuple(done)


def from_behind(value, axis, steps):
    count = lax.axis_size(axis)
    leading, last = (max(0, -steps), min(count, count - steps))
    return lax.ppermute(value, axis, [(source, source + steps) for source in range(leading, last)])


def split_up(shard, dim, peers):
    before, after = (shard.shape[:dim], shard.shape[dim + 1 :])
    return jnp.moveaxis(shard.reshape(*before, peers, -1, *after), dim, 0)


def sent_and_summed(shard, axis, dim):
    blocks = split_up(shard, dim, lax.axis_size(axis))
    arrived = lax.all_to_all(blocks, axis, split_axis=0, concat_axis=0, tiled=True)
    return arrived.sum(axis=0)


def rows_for(lines, peers):
    spare = -len(lines) % peers
    return jnp.pad(lines, [(0, spare)] + [(0, 0)] * (lines.ndim - 1))


def copy_for_each(shard, axis):
    copies = jnp.broadcast_to(shard, (lax.axis_size(axis), *shard.shape))
    return lax.all_to_all(copies, axis, split_axis=0, concat_axis=0, tiled=True)


def joined_along(blocks, dim):
    blocks = jnp.moveaxis(blocks, 0, dim)
    lengths = blocks.shape
    return blocks.reshape(*lengths[:dim], lengths[dim] * lengths[dim + 1], *lengths[dim + 2 :])


def gather_directly(shard, axis, dim):
    blocks = copy_for_each(shard, axis)
    return joined_along(blocks, dim)


def nested_sum(shard, axes):
    lines = shard.reshape(-1, shard.shape[-1])
    own = sent_and_summed(rows_for(lines, lax.axis_size(axes)), axes, 0)
    whole = gather_directly(own, axes, 0)
    return whole[: len(lines)].reshape(shard.shape)


def taken_together(shard, axis):
    everything = copy_for_each(shard, axis)
    return jnp.sum(everything, axis=0)


def packed_total(arrays, axis):
    ends = [0]
    for a in arrays:
        ends.append(ends[-1] + a.size)
    subtotal = taken_together(jnp.concatenate([a.ravel() for a in arrays]), axis)
    return tuple((subtotal[b:e].reshape(a.shape) for a, b, e in zip(arrays, ends, ends[1:])))


def apply_terms(left_ops, right_ops, my_charges, own, lower, upper):
    stacked = jnp.stack([upper, own, lower])
    picked = stacked[my_charges + 1]
    inner = jnp.einsum(
        "tij,tjk->tik", left_ops[:, 0], picked, preferred_element_type=jnp.float32
    ).astype(jnp.bfloat16)
    image = jnp.einsum("tij,tkj->tik", inner, right_ops[:, 0], preferred_element_type=jnp.float32)
    return jnp.sum(image, axis=0)


def per_device(wave, left_ops, right_ops, charges, diag):
    per_dev = left_ops.shape[0]
    my_charges = lax.dynamic_slice_in_dim(charges, lax.axis_index("term") * per_dev, per_dev)
    psi, full_diag = sent_together((wave[0], diag[0]), "term", 0, 1)
    for step in range(STEPS):
        wb = psi.astype(jnp.bfloat16)
        lower = from_behind(wb, "sector", 1)
        upper = from_behind(wb, "sector", -1)
        partial_image = apply_terms(left_ops, right_ops, my_charges, wb, lower, upper)
        hpsi = nested_sum(partial_image, "term")
        cross, square = packed_total((jnp.sum(psi * hpsi), jnp.sum(psi * psi)), "sector")
        theta = cross / square
        fresh = psi - (hpsi - theta * psi) / jnp.maximum(jnp.abs(full_diag - theta), 1.0)
        total = taken_together(jnp.sum(fresh * fresh), "sector")
        psi = fresh / jnp.sqrt(total / (lax.axis_size("sector") * fresh.size) + 1e-06)
    rows_dev = wave.shape[1]
    result = lax.dynamic_slice_in_dim(psi, lax.axis_index("term") * rows_dev, rows_dev, 0)
    return result[None]


def solution(mesh):
    in_specs = (
        P("sector", "term", None),
        P("term", "sector", None, None),
        P("term", "sector", None, None),
        P(),
        P("sector", "term", None),
    )
    out_specs = P("sector", "term", None)
    return jax.shard_map(
        per_device, mesh=mesh, in_specs=in_specs, out_specs=out_specs, check_vma=False
    )
```

profile of v0, /device:TPU:1, one launch (start us, length us, event | category | flops | bytes accessed | tf_op | source)
XLA Modules:
  0.0 513.6 jit_solution(6668735653147404938)
XLA Ops:
  8.2 109.2 %all-gather.2.cloned.1.call-done = f32[512,1024]{1,0:T(8,128)} async-done(((f32[32,1024]{1,0:T(8,128)}), f32[512,1024]{1,0:T(8,128)}) %all-gather.2.cloned.1.call-update) | async-done | bytes 2097168 | tf_op jit(solution)/shard_map/all_gather | solution.py:11
  118.7 8.6 %collective-permute-start.1 = (bf16[512,512]{1,0:T(8,128)(2,1)S(1)}, bf16[512,512]{1,0:T(8,128)(2,1)S(1)}, u32[]{:S(2)}, u32[]{:S(2)}) collective-permute-start(bf16[512,512]{1,0:T(8,128)(2,1)S(1)} %slice.47), channel_id=1, source_target_pairs={{0,16},{16,32},{32,48},{48,64},{64,80},{80,96},{96,112},{112,128},... | collective-permute-start | bytes 1572872 | tf_op jit(solution)/shard_map/ppermute | solution.py:21
  133.4 4.5 collective-permute-done
  138.0 2.4 pad_maximum_fusion
  140.3 3.4 gather_fusion
  143.7 3.0 fusion.18
  148.0 29.0 %all_to_all.66 = f32[16,32,512]{2,1,0:T(8,128)S(1)} all-to-all(f32[16,32,512]{2,1,0:T(8,128)S(1)} %fusion.21), channel_id=1, replica_groups=mesh['sector'=32,'term'=16] {'term'}, dimensions={0} | all-to-all | bytes 2097152 | tf_op jit(solution)/shard_map/all_to_all | solution.py:31
  177.2 32.4 %all_to_all.67 = f32[16,32,512]{2,1,0:T(8,128)S(1)} all-to-all(f32[16,32,512]{2,1,0:T(8,128)S(1)} %broadcast_in_dim.36), channel_id=1, replica_groups=mesh['sector'=32,'term'=16] {'term'}, dimensions={0} | all-to-all | bytes 2097152 | tf_op jit(solution)/shard_map/all_to_all | solution.py:42
  211.9 22.0 %all_to_all.68 = f32[32,1,2]{2,1,0:T(1,128)S(1)} all-to-all(f32[32,1,2]{2,1,0:T(1,128)S(1)} %broadcast_in_dim.37), channel_id=1, replica_groups=mesh['sector'=32,'term'=16] {'sector'}, dimensions={0} | all-to-all | bytes 512 | tf_op jit(solution)/shard_map/all_to_all | solution.py:42
  235.7 2.8 multiply_reduce_fusion.4
  239.1 10.7 %all_to_all.69 = f32[32,1,1]{2,1,0:T(1,128)S(1)} all-to-all(f32[32,1,1]{2,1,0:T(1,128)S(1)} %broadcast_in_dim.38), channel_id=1, replica_groups=mesh['sector'=32,'term'=16] {'sector'}, dimensions={0} | all-to-all | bytes 256 | tf_op jit(solution)/shard_map/all_to_all | solution.py:42
  251.3 2.7 collective-permute-start.3
  256.1 4.0 collective-permute-done.3
  260.1 4.4 collective-permute-done.2
  265.9 3.4 gather_fusion.1
  269.3 3.0 fusion.15
  273.5 30.1 %all_to_all.70 = f32[16,32,512]{2,1,0:T(8,128)} all-to-all(f32[16,32,512]{2,1,0:T(8,128)S(1)} %fusion.24), channel_id=1, replica_groups=mesh['sector'=32,'term'=16] {'term'}, dimensions={0} | all-to-all | bytes 2097152 | tf_op jit(solution)/shard_map/all_to_all | solution.py:31
  305.1 32.1 %all_to_all.71 = f32[16,32,512]{2,1,0:T(8,128)S(1)} all-to-all(f32[16,32,512]{2,1,0:T(8,128)S(1)} %broadcast_in_dim.39), channel_id=1, replica_groups=mesh['sector'=32,'term'=16] {'term'}, dimensions={0} | all-to-all | bytes 2097152 | tf_op jit(solution)/shard_map/all_to_all | solution.py:42
  339.4 20.0 %all_to_all.72 = f32[32,1,2]{2,1,0:T(1,128)S(1)} all-to-all(f32[32,1,2]{2,1,0:T(1,128)S(1)} %broadcast_in_dim.40), channel_id=1, replica_groups=mesh['sector'=32,'term'=16] {'sector'}, dimensions={0} | all-to-all | bytes 512 | tf_op jit(solution)/shard_map/all_to_all | solution.py:42
  361.3 2.8 multiply_reduce_fusion.2
  364.7 10.7 %all_to_all.73 = f32[32,1,1]{2,1,0:T(1,128)S(1)} all-to-all(f32[32,1,1]{2,1,0:T(1,128)S(1)} %broadcast_in_dim.41), channel_id=1, replica_groups=mesh['sector'=32,'term'=16] {'sector'}, dimensions={0} | all-to-all | bytes 256 | tf_op jit(solution)/shard_map/all_to_all | solution.py:42
  376.9 2.7 collective-permute-start.5
  381.8 3.9 collective-permute-done.5
  385.7 4.4 collective-permute-done.4
  391.5 3.4 gather_fusion.2
  394.8 3.0 fusion.12
  399.1 30.0 %all_to_all.74 = f32[16,32,512]{2,1,0:T(8,128)} all-to-all(f32[16,32,512]{2,1,0:T(8,128)S(1)} %fusion.27), channel_id=1, replica_groups=mesh['sector'=32,'term'=16] {'term'}, dimensions={0} | all-to-all | bytes 2097152 | tf_op jit(solution)/shard_map/all_to_all | solution.py:31
  430.5 32.1 %all_to_all.75 = f32[16,32,512]{2,1,0:T(8,128)S(1)} all-to-all(f32[16,32,512]{2,1,0:T(8,128)S(1)} %broadcast_in_dim.42), channel_id=1, replica_groups=mesh['sector'=32,'term'=16] {'term'}, dimensions={0} | all-to-all | bytes 2097152 | tf_op jit(solution)/shard_map/all_to_all | solution.py:42
  465.7 20.0 %all_to_all.76 = f32[32,1,2]{2,1,0:T(1,128)S(1)} all-to-all(f32[32,1,2]{2,1,0:T(1,128)S(1)} %broadcast_in_dim.43), channel_id=1, replica_groups=mesh['sector'=32,'term'=16] {'sector'}, dimensions={0} | all-to-all | bytes 512 | tf_op jit(solution)/shard_map/all_to_all | solution.py:42
  487.7 3.5 multiply_reduce_fusion
  492.4 4.1 all-to-all-start.11
  496.5 7.4 %all-to-all-done.11 = f32[32,1,1]{2,1,0:T(1,128)S(1)} async-done(((f32[32,1,1]{2,1,0:T(1,128)}), f32[32,1,1]{2,1,0:T(1,128)S(1)}, u32[]{:S(2)}, u32[]{:S(2)}) %all-to-all-start.11) | async-done | bytes 160 | tf_op jit(solution)/shard_map/all_to_all | solution.py:42
  (66 shorter events, 38.4 us)
Async XLA Ops:
  6.5 137.2 %copy-start = (bf16[4,1,512,512]{3,2,1,0:T(8,128)(2,1)S(1)}, bf16[4,1,512,512]{3,2,1,0:T(8,128)(2,1)}, u32[]{:S(2)}) copy-start(bf16[4,1,512,512]{3,2,1,0:T(8,128)(2,1)} %param.6) | copy-start | bytes 6291460
  6.5 110.9 %all-gather.2.cloned.1.call-start = ((), (), s32[]{:S(2)}) async-start(), calls=%async_computation.12 | async-start | bytes 2228224 | tf_op jit(solution)/shard_map/all_gather | solution.py:11
  118.7 14.7 %collective-permute-start.1 = (bf16[512,512]{1,0:T(8,128)(2,1)S(1)}, bf16[512,512]{1,0:T(8,128)(2,1)S(1)}, u32[]{:S(2)}, u32[]{:S(2)}) collective-permute-start(bf16[512,512]{1,0:T(8,128)(2,1)S(1)} %slice.47), channel_id=1, source_target_pairs={{0,16},{16,32},{32,48},{48,64},{64,80},{80,96},{96,112},{112,128},... | collective-permute-start | bytes 1572872 | tf_op jit(solution)/shard_map/ppermute | solution.py:21
  127.3 10.6 %collective-permute-start = (bf16[512,512]{1,0:T(8,128)(2,1)S(1)}, bf16[512,512]{1,0:T(8,128)(2,1)}, u32[]{:S(2)}, u32[]{:S(2)}) collective-permute-start(bf16[512,512]{1,0:T(8,128)(2,1)S(1)} %slice.47), channel_id=1, source_target_pairs={{16,0},{32,16},{48,32},{64,48},{80,64},{96,80},{112,96},{128,112},... | collective-permute-start | bytes 1572872 | tf_op jit(solution)/shard_map/ppermute | solution.py:21
  143.7 3.0 copy-start.6
  177.1 32.5 %copy-start.2 = (f32[512,1024]{1,0:T(8,128)S(1)}, f32[512,1024]{1,0:T(8,128)}, u32[]{:S(2)}) copy-start(f32[512,1024]{1,0:T(8,128)} %all-gather.2.cloned.1.call-done) | copy-start | bytes 6291460
  209.6 1.0 copy-start.5
  238.6 98.6 %copy-start.1 = (f32[512,512]{1,0:T(8,128)}, f32[512,512]{1,0:T(8,128)S(1)}, u32[]{:S(2)}) copy-start(f32[512,512]{1,0:T(8,128)S(1)} %get-tuple-element.16) | copy-start | bytes 3145732
  251.3 8.8 %collective-permute-start.3 = (bf16[512,512]{1,0:T(8,128)(2,1)S(1)}, bf16[512,512]{1,0:T(8,128)(2,1)S(1)}, u32[]{:S(2)}, u32[]{:S(2)}) collective-permute-start(bf16[512,512]{1,0:T(8,128)(2,1)S(1)} %fusion.40), channel_id=1, source_target_pairs={{0,16},{16,32},{32,48},{48,64},{64,80},{80,96},{96,112},{112,128},... | collective-permute-start | bytes 1572872 | tf_op jit(solution)/shard_map/ppermute | solution.py:21
  254.0 10.5 %collective-permute-start.2 = (bf16[512,512]{1,0:T(8,128)(2,1)S(1)}, bf16[512,512]{1,0:T(8,128)(2,1)S(1)}, u32[]{:S(2)}, u32[]{:S(2)}) collective-permute-start(bf16[512,512]{1,0:T(8,128)(2,1)S(1)} %fusion.40), channel_id=1, source_target_pairs={{16,0},{32,16},{48,32},{64,48},{80,64},{96,80},{112,96},{128,112},... | collective-permute-start | bytes 1572872 | tf_op jit(solution)/shard_map/ppermute | solution.py:21
  269.3 3.0 copy-start.7
  337.1 1.0 copy-start.4
  376.9 8.8 %collective-permute-start.5 = (bf16[512,512]{1,0:T(8,128)(2,1)S(1)}, bf16[512,512]{1,0:T(8,128)(2,1)S(1)}, u32[]{:S(2)}, u32[]{:S(2)}) collective-permute-start(bf16[512,512]{1,0:T(8,128)(2,1)S(1)} %fusion.41), channel_id=1, source_target_pairs={{0,16},{16,32},{32,48},{48,64},{64,80},{80,96},{96,112},{112,128},... | collective-permute-start | bytes 1572872 | tf_op jit(solution)/shard_map/ppermute | solution.py:21
  379.6 10.5 %collective-permute-start.4 = (bf16[512,512]{1,0:T(8,128)(2,1)S(1)}, bf16[512,512]{1,0:T(8,128)(2,1)S(1)}, u32[]{:S(2)}, u32[]{:S(2)}) collective-permute-start(bf16[512,512]{1,0:T(8,128)(2,1)S(1)} %fusion.41), channel_id=1, source_target_pairs={{16,0},{32,16},{48,32},{64,48},{80,64},{96,80},{112,96},{128,112},... | collective-permute-start | bytes 1572872 | tf_op jit(solution)/shard_map/ppermute | solution.py:21
  394.8 3.0 copy-start.8
  462.6 1.0 copy-start.3
  492.4 11.5 %all-to-all-start.11 = ((f32[32,1,1]{2,1,0:T(1,128)}), f32[32,1,1]{2,1,0:T(1,128)S(1)}, u32[]{:S(2)}, u32[]{:S(2)}) async-start(f32[32,1,1]{2,1,0:T(1,128)} %broadcast_in_dim.44), calls=%async_computation.11 | async-start | bytes 32768 | tf_op jit(solution)/shard_map/all_to_all | solution.py:42
Sparse Core Ops, SparseCore 0:
  10.5 106.8 all-gather.1
where the time goes:
time: 515 us; the launch traced here: 514 us
  blocking collectives  269 us (52%)
  waiting for transfers between devices  140 us (27%)
  other arithmetic  29.8 us (6%)
  starting transfers between devices  24.2 us (5%)
  between operations  19.4 us (4%)
  local copies, waits for them, and re-layouts  18.4 us (4%)
  matrix products  12.8 us (2%)
    all_to_all x8, blocking collectives, copy_for_each(): return lax.all_to_all(copies, axis, split_axis=0, concat_axis=0, tiled=True)  180 us
    all_gather x1, waiting for transfers between devices, sent_together(): result, at, done = (lax.all_gather(both, axis, axis=dim, tiled=True), 0, [])  109 us
    all_to_all x3, blocking collectives, sent_and_summed(): lax.all_to_all(blocks, axis, split_axis=0, concat_axis=0, tiled=True)  89.1 us
    ppermute x6, waiting for transfers between devices, from_behind(): lax.ppermute(value, axis, [(source, source + steps) for source in range(l...  23.3 us
    ppermute x6, starting transfers between devices, from_behind(): lax.ppermute(value, axis, [(source, source + steps) for source in range(l...  20 us
  transfers between devices with their start and end apart: 8, of which 8 were waited for; matrix products, arithmetic and copies ran while one was open for 0% of the time, Pallas kernels for 0%

commit v1 on v0

v1 whole, which is shorter than its diff:
```python
import functools

import jax
import jax.numpy as jnp
from jax import lax
from jax.experimental import pallas as pl
from jax.experimental.pallas import tpu as pltpu
from jax.sharding import PartitionSpec as P

STEPS = 3
ROWS = 32
BF16, F32 = jnp.bfloat16, jnp.float32
LONG = ((0, 0), (1, 1))
SHORT = ((0, 1), (1, 0))


def wrapped(value, count):
    return lax.rem(value + count, count)


def lane_sums(x):
    x = jnp.sum(x, axis=0, keepdims=True)
    return x[:, :128] + x[:, 128:256] + x[:, 256:384] + x[:, 384:]


def kernel(
    total_size,
    charges,
    wave,
    diag,
    left_hbm,
    right_hbm,
    out,
    left,
    right,
    blocks,
    image,
    rs_out,
    rs_in,
    z_out,
    z_in,
    f,
    dg,
    sc_out,
    sc_in,
    load_sem,
    first_send,
    first_recv,
    ag_send,
    ag_recv,
    nb_send,
    nb_recv,
    rs_send,
    rs_recv,
    z_send,
    z_recv,
    sc_send,
    sc_recv,
):
    s, t = lax.axis_index("sector"), lax.axis_index("term")
    sectors = lax.axis_size("sector")
    y, zh = lax.rem(t, 8), lax.div(t, 8)
    xc, zl = lax.rem(s, 8), lax.div(s, 8)
    z = zh * 4 + zl

    def remote(src, dst, send, recv, sector, term):
        return pltpu.make_async_remote_copy(
            src_ref=src,
            dst_ref=dst,
            send_sem=send,
            recv_sem=recv,
            device_id={"sector": sector, "term": term},
            device_id_type=pl.DeviceIdType.MESH,
        )

    def arrived(ref, sem):
        pltpu.make_async_copy(ref, ref, sem).wait()

    def peer(phase, offset):
        if phase == 0:
            return s, zh * 8 + lax.rem(y + offset, 8)
        if phase == 1:
            return zl * 8 + lax.rem(xc + offset, 8), t
        other = lax.rem(z + offset, 8)
        return lax.rem(other, 4) * 8 + xc, lax.div(other, 4) * 8 + y

    place = (y, xc, z)
    has_lower, has_upper = s > 0, s < sectors - 1

    loads = [
        pltpu.make_async_copy(left_hbm, left, load_sem.at[0]),
        pltpu.make_async_copy(right_hbm, right, load_sem.at[1]),
    ]
    for load in loads:
        load.start()

    barrier = pltpu.get_barrier_semaphore()

    def greet(sector, term):
        pl.semaphore_signal(
            barrier,
            inc=1,
            device_id={"sector": sector, "term": term},
            device_id_type=pl.DeviceIdType.MESH,
        )

    for phase in range(3):
        for offset in range(1, 8):
            greet(*peer(phase, offset))
    far_lower = jnp.logical_and(xc == 0, has_lower)
    far_upper = jnp.logical_and(xc == 7, has_upper)

    @pl.when(far_lower)
    def _():
        greet(s - 1, t)

    @pl.when(far_upper)
    def _():
        greet(s + 1, t)

    f[zh] = wave[0]
    dg[zh] = diag[0]
    blocks[0, 1, zh, y] = wave[0].astype(BF16)

    @pl.when(s == 0)
    def _():
        for k in range(STEPS):
            blocks[k, 2] = jnp.zeros(blocks.shape[2:], BF16)

    @pl.when(s == sectors - 1)
    def _():
        for k in range(STEPS):
            blocks[k, 0] = jnp.zeros(blocks.shape[2:], BF16)

    first_square = lane_sums(jnp.square(wave[0]))
    pl.semaphore_wait(barrier, 21 + far_lower.astype(jnp.int32) + far_upper.astype(jnp.int32))

    zt = (1 - zh) * 8 + y
    ring_to = (zh * 8 + wrapped(y + 1, 8), zh * 8 + wrapped(y - 1, 8))
    first = [
        remote(blocks.at[0, 1, zh, y], blocks.at[0, 1, zh, y], first_send.at[0], first_recv.at[0], s, zt),
        remote(wave.at[0], f.at[zh], first_send.at[1], first_recv.at[1], s, zt),
        remote(diag.at[0], dg.at[zh], first_send.at[2], first_recv.at[2], s, zt),
    ]
    for copy in first:
        copy.start()
    first[0].wait_recv()

    def position(d, distance):
        return wrapped(y - distance if d == 0 else y + distance, 8)

    def destination(d, distance):
        return wrapped(y + distance if d == 0 else y - distance, 8)

    def hand_on(k, ref_of):
        @pl.when(has_upper)
        def _():
            remote(ref_of(blocks.at[k, 1]), ref_of(blocks.at[k, 2]), nb_send.at[0], nb_recv.at[k, 0], s + 1, t).start()

        @pl.when(has_lower)
        def _():
            remote(ref_of(blocks.at[k, 1]), ref_of(blocks.at[k, 0]), nb_send.at[1], nb_recv.at[k, 1], s - 1, t).start()

    def gather(k):
        def ring_copy(d, h, r):
            piece = blocks.at[k, 1, h, position(d, r)]
            return remote(piece, piece, ag_send.at[0], ag_recv.at[k, d, h, r], s, ring_to[d])

        def wait_piece(d, h, r):
            ring_copy(d, h, r).wait_recv()

        for r in range(4):
            for d, h in LONG:
                if r:
                    wait_piece(d, h, r - 1)
                ring_copy(d, h, r).start()
            for d, h in SHORT:
                if r:
                    wait_piece(d, h, r - 1)
                if r < 3:
                    ring_copy(d, h, r).start()
            hand_on(k, lambda ref: ref.at[:, position(0, r)])
            if r:
                hand_on(k, lambda ref: ref.at[:, position(1, r)])
        for d, h in LONG:
            wait_piece(d, h, 3)
        hand_on(k, lambda ref: ref.at[:, position(0, 4)])

        @pl.when(has_lower)
        def _():
            arrived(blocks.at[k, 2], nb_recv.at[k, 0])

        @pl.when(has_upper)
        def _():
            arrived(blocks.at[k, 0], nb_recv.at[k, 1])

    def apply_rows(k, ends):
        total = None
        for i in range(4):
            source = blocks[k, charges[t * 4 + i] + 1].reshape(512, 512)
            rows = jnp.concatenate([left[i, h, e] for e in ends for h in range(2)], axis=0)
            inner = jnp.dot(rows, source, preferred_element_type=F32).astype(BF16)
            term = lax.dot_general(inner, right[i], (((1,), (1,)), ((), ())), preferred_element_type=F32)
            total = term if total is None else total + term
        mine = jnp.concatenate([blocks[k, 1, h, e] for e in ends for h in range(2)], axis=0)
        for j, e in enumerate(ends):
            for h in range(2):
                at = (2 * j + h) * ROWS
                image[h, e] = total[at : at + ROWS]
        return lane_sums(total * mine.astype(F32))

    def pass_on(k, d, h, q):
        where = destination(d, q)
        value = image[h, where]
        if q < (4 if (d, h) in LONG else 3):
            rs_copy(k, d, h, q + 1).wait_recv()
            value = value + rs_in[k, d, h, q].astype(F32)
        rs_out[k, d, h, q - 1] = value.astype(BF16)
        rs_copy(k, d, h, q).start()

    def rs_copy(k, d, h, q):
        return remote(
            rs_out.at[k, d, h, q - 1],
            rs_in.at[k, d, h, q - 1],
            rs_send.at[0],
            rs_recv.at[k, d, h, q - 1],
            s,
            ring_to[d],
        )

    def sum_start(k, phase, values):
        sc_out[k, phase] = values
        sc_in[k, phase, place[phase]] = values
        for offset in range(1, 8):
            remote(
                sc_out.at[k, phase],
                sc_in.at[k, phase, place[phase]],
                sc_send.at[0],
                sc_recv.at[k, phase],
                *peer(phase, offset),
            ).start()

    def sum_end(k, phase):
        arrived(sc_in.at[k, phase, pl.ds(0, 7)], sc_recv.at[k, phase])
        return jnp.sum(sc_in[k, phase], axis=0)

    def pair(cross, square):
        return jnp.concatenate([cross, square], axis=0)

    def step(k, square):
        gather(k)

        @pl.when(k == 0)
        def _():
            for load in loads:
                load.wait()

        cross = apply_rows(k, (destination(0, 4), destination(0, 3)))
        for d, h in LONG:
            pass_on(k, d, h, 4)
        pass_on(k, 0, 1, 3)
        cross += apply_rows(k, (destination(1, 3), destination(0, 2)))
        pass_on(k, 1, 0, 3)
        cross += apply_rows(k, (destination(1, 2), destination(0, 1)))
        for d, h in LONG:
            pass_on(k, d, h, 3)
        cross += apply_rows(k, (destination(1, 1), y))
        sum_start(k, 0, pair(cross, square))
        for d, h in SHORT + LONG:
            pass_on(k, d, h, 2)
        sum_start(k, 1, sum_end(k, 0))
        for d, h in SHORT + LONG:
            pass_on(k, d, h, 1)
        for h in range(2):
            for d in range(2):
                rs_copy(k, d, h, 1).wait_recv()
            z_out[k, h] = (image[h, y] + rs_in[k, 0, h, 0].astype(F32) + rs_in[k, 1, h, 0].astype(F32)).astype(BF16)
        across = remote(z_out.at[k], z_in.at[k], z_send.at[0], z_recv.at[k], s, zt)
        across.start()
        sum_start(k, 2, sum_end(k, 1))
        sums = sum_end(k, 2)
        both = jnp.sum(sums, axis=1, keepdims=True)
        cross_total, square_total = both[0:1], both[1:2]
        theta = (cross_total / square_total)[None]
        scale = jnp.where(k == 0, 1.0, 1.0 / jnp.sqrt(square_total / total_size + 1e-06))[None]

        @pl.when(k == 0)
        def _():
            first[1].wait_recv()
            first[2].wait_recv()

        across.wait_recv()
        hpsi = (z_out[k].astype(F32) + z_in[k].astype(F32)) * scale
        psi = f[...] * scale
        fresh = psi - (hpsi - theta * psi) / jnp.maximum(jnp.abs(dg[...] - theta), 1.0)
        f[...] = fresh

        @pl.when(k < STEPS - 1)
        def _():
            blocks[jnp.minimum(k + 1, STEPS - 1), 1, :, y] = fresh.astype(BF16)

        return 0.5 * lane_sums(jnp.square(fresh).reshape(2 * ROWS, 512))

    square = lax.fori_loop(0, STEPS, step, first_square)
    last = pair(square, square)
    for phase in range(3):
        sum_start(STEPS, phase, last)
        last = sum_end(STEPS, phase)
    norm = jnp.sum(last, axis=1, keepdims=True)[1:2]
    out[0] = f[zh] / jnp.sqrt(norm / total_size + 1e-06)

    for copy in first:
        copy.wait_send()
    arrived(rs_in.at[:, :, :, pl.ds(0, 3)], ag_send.at[0])
    arrived(rs_in.at[:, 0, :, pl.ds(0, 1)], ag_send.at[0])
    arrived(rs_in.at[:, :, :, pl.ds(0, 3)], rs_send.at[0])
    arrived(rs_in.at[:, 0, :, pl.ds(0, 1)], rs_send.at[0])
    arrived(z_in, z_send.at[0])
    arrived(sc_in.at[:, :, pl.ds(0, 7)], sc_send.at[0])

    @pl.when(has_upper)
    def _():
        arrived(blocks.at[:, 0], nb_send.at[0])

    @pl.when(has_lower)
    def _():
        arrived(blocks.at[:, 0], nb_send.at[1])


def per_device(wave, left_ops, right_ops, charges, diag):
    total_size = float(lax.axis_size("sector") * 512 * 512)
    vmem = pl.BlockSpec(memory_space=pltpu.VMEM)
    hbm = pl.BlockSpec(memory_space=pl.ANY)
    dma = pltpu.SemaphoreType.DMA
    return pl.pallas_call(
        functools.partial(kernel, total_size),
        out_shape=jax.ShapeDtypeStruct(wave.shape, F32),
        in_specs=[pl.BlockSpec(memory_space=pltpu.SMEM), vmem, vmem, hbm, hbm],
        out_specs=vmem,
        scratch_shapes=[
            pltpu.VMEM((4, 2, 8, ROWS, 512), BF16),
            pltpu.VMEM((4, 512, 512), BF16),
            pltpu.VMEM((STEPS, 3, 2, 8, ROWS, 512), BF16),
            pltpu.VMEM((2, 8, ROWS, 512), F32),
            pltpu.VMEM((STEPS, 2, 2, 4, ROWS, 512), BF16),
            pltpu.VMEM((STEPS, 2, 2, 4, ROWS, 512), BF16),
            pltpu.VMEM((STEPS, 2, ROWS, 512), BF16),
            pltpu.VMEM((STEPS, 2, ROWS, 512), BF16),
            pltpu.VMEM((2, ROWS, 512), F32),
            pltpu.VMEM((2, ROWS, 512), F32),
            pltpu.VMEM((STEPS + 1, 3, 2, 128), F32),
            pltpu.VMEM((STEPS + 1, 3, 8, 2, 128), F32),
            dma((2,)),
            dma((3,)),
            dma((3,)),
            dma((1,)),
            dma((STEPS, 2, 2, 4)),
            dma((2,)),
            dma((STEPS, 2)),
            dma((1,)),
            dma((STEPS, 2, 2, 4)),
            dma((1,)),
            dma((STEPS,)),
            dma((1,)),
            dma((STEPS + 1, 3)),
        ],
        compiler_params=pltpu.CompilerParams(
            collective_id=0, has_side_effects=True, vmem_limit_bytes=48 * 1024 * 1024
        ),
        name="sweep",
    )(
        charges,
        wave,
        diag,
        left_ops.reshape(4, 2, 8, ROWS, 512),
        right_ops.reshape(4, 512, 512),
    )


def solution(mesh):
    in_specs = (
        P("sector", "term", None),
        P("term", "sector", None, None),
        P("term", "sector", None, None),
        P(),
        P("sector", "term", None),
    )
    out_specs = P("sector", "term", None)
    return jax.shard_map(
        per_device, mesh=mesh, in_specs=in_specs, out_specs=out_specs, check_vma=False
    )
```

time: 515 us -> 147 us (0.29)
  blocking collectives: 269 us -> 0 us
  Pallas kernels: 0 us -> 140 us
  waiting for transfers between devices: 140 us -> 0 us
  other arithmetic: 29.8 us -> 0 us
  starting transfers between devices: 24.2 us -> 0 us
  between operations: 19.4 us -> 0.01 us
  matrix products: 12.8 us -> 0 us
  local copies, waits for them, and re-layouts: 18.4 us -> 6.15 us
    all_to_all x11 -> x0, blocking collectives: 269 us -> none  [the longest x8 180 us: copy_for_each(): return lax.all_to_all(copies, axis, split_axis=0, concat_axis=0, tiled=True)]
    pallas_call x0 -> x1, Pallas kernels: none -> 140 us  [per_device(): pl.pallas_call(functools.partial(kernel, total_size), out_shape=jax.Shape...]
    all_gather x1 -> x0, waiting for transfers between devices: 109 us -> none  [sent_together(): result, at, done = (lax.all_gather(both, axis, axis=dim, tiled=True), 0, [])]
    ppermute x6 -> x0, waiting for transfers between devices: 23.3 us -> none  [from_behind(): lax.ppermute(value, axis, [(source, source + steps) for source in range(l...]
    ppermute x6 -> x0, starting transfers between devices: 20 us -> none  [from_behind(): lax.ppermute(value, axis, [(source, source + steps) for source in range(l...]
    reduce_sum x15 -> x0, other arithmetic: 16.5 us -> none  [the longest x3 9.15 us: per_device(): total = taken_together(jnp.sum(fresh * fresh), 'sector')]
    dot_general x6 -> x0, matrix products: 12.8 us -> none  [the longest x3 8.97 us: apply_terms(): jnp.einsum('tij,tjk->tik', left_ops[:, 0], picked, preferred_element_type...]
    gather x3 -> x0, local copies, waits for them, and re-layouts: 10.1 us -> none  [apply_terms(): picked = stacked[my_charges + 1]]
  transfers between devices with their start and end apart: 8 -> 0, of which waited for: 8 -> 0; matrix products, arithmetic and copies ran while one was open for 0% -> 0% of each run, Pallas kernels for 0% -> 0%
where the time goes in v1:
time: 147 us
  Pallas kernels  140 us (95%)
  local copies, waits for them, and re-layouts  6.15 us (4%)
    pallas_call x1, Pallas kernels, per_device(): pl.pallas_call(functools.partial(kernel, total_size), out_shape=jax.Shape...  140 us
    unnamed x11, local copies, waits for them, and re-layouts  6.15 us

profile of v1, /device:TPU:1, one launch (start us, length us, event | category | flops | bytes accessed | tf_op | source)
XLA Modules:
  0.0 146.6 jit_solution(5513747881597718085)
XLA Ops:
  0.0 0.0 copy-start
  0.0 1.6 %copy-done = bf16[4,1,512,512]{3,2,1,0:T(8,128)(2,1)S(1)} copy-done((bf16[4,1,512,512]{3,2,1,0:T(8,128)(2,1)S(1)}, bf16[4,1,512,512]{3,2,1,0:T(8,128)(2,1)}, u32[]{:S(2)}) %copy-start) | copy-done | bytes 2097176
  1.6 0.0 copy-start.1
  1.6 1.6 %copy-done.1 = bf16[4,1,512,512]{3,2,1,0:T(8,128)(2,1)S(1)} copy-done((bf16[4,1,512,512]{3,2,1,0:T(8,128)(2,1)S(1)}, bf16[4,1,512,512]{3,2,1,0:T(8,128)(2,1)}, u32[]{:S(2)}) %copy-start.1) | copy-done | bytes 2097176
  3.2 0.0 copy-start.2
  3.2 0.8 copy-done.2
  4.0 0.0 copy-start.3
  4.0 0.8 copy-done.3
  4.9 0.0 copy-start.4
  4.9 0.7 copy-done.4
  5.5 140.5 %sweep.1 = f32[1,32,512]{2,1,0:T(8,128)S(1)} custom-call(s32[64]{0:T(128)S(1)} %copy-done.4, f32[1,32,512]{2,1,0:T(8,128)S(1)} %copy-done.2, f32[1,32,512]{2,1,0:T(8,128)S(1)} %copy-done.3, bf16[4,2,8,32,512]{4,3,2,1,0:T(8,128)(2,1)S(1)} %bitcast.2, bf16[4,512,512]{2,1,0:T(8,128)(2,1)S(1)} %bitcast.3), custom_call_target="tpu_custom_call" | custom-call | tf_op jit(solution)/shard_map/sweep/pallas_call | solution.py:335
  146.0 0.6 copy.7
Async XLA Ops:
  0.0 1.6 %copy-start = (bf16[4,1,512,512]{3,2,1,0:T(8,128)(2,1)S(1)}, bf16[4,1,512,512]{3,2,1,0:T(8,128)(2,1)}, u32[]{:S(2)}) copy-start(bf16[4,1,512,512]{3,2,1,0:T(8,128)(2,1)} %param.6) | copy-start | bytes 6291460
  1.6 1.6 %copy-start.1 = (bf16[4,1,512,512]{3,2,1,0:T(8,128)(2,1)S(1)}, bf16[4,1,512,512]{3,2,1,0:T(8,128)(2,1)}, u32[]{:S(2)}) copy-start(bf16[4,1,512,512]{3,2,1,0:T(8,128)(2,1)} %param.7) | copy-start | bytes 6291460
  3.2 0.8 copy-start.2
  4.0 0.8 copy-start.3
  4.9 0.7 copy-start.4

commit v2 on v1

--- a/solution.py
+++ b/solution.py
@@ -8,6 +8,7 @@
 from jax.sharding import PartitionSpec as P
 
 STEPS = 3
+SLOTS = (16, 32)
 ROWS = 32
 BF16, F32 = jnp.bfloat16, jnp.float32
 LONG = ((0, 0), (1, 1))
@@ -26,8 +27,8 @@
 def kernel(
     total_size,
     charges,
-    wave,
-    diag,
+    wave_hbm,
+    diag_hbm,
     left_hbm,
     right_hbm,
     out,
@@ -42,7 +43,8 @@
     f,
     dg,
     sc_out,
-    sc_in,
+    sc_in_0,
+    sc_in_1,
     load_sem,
     first_send,
     first_recv,
@@ -60,8 +62,10 @@
     s, t = lax.axis_index("sector"), lax.axis_index("term")
     sectors = lax.axis_size("sector")
     y, zh = lax.rem(t, 8), lax.div(t, 8)
-    xc, zl = lax.rem(s, 8), lax.div(s, 8)
+    core, x, zl = lax.rem(s, 2), lax.rem(lax.div(s, 2), 4), lax.div(s, 8)
     z = zh * 4 + zl
+
+    sc_in = (sc_in_0, sc_in_1)
 
     def remote(src, dst, send, recv, sector, term):
         return pltpu.make_async_remote_copy(
@@ -78,20 +82,24 @@
 
     def peer(phase, offset):
         if phase == 0:
-            return s, zh * 8 + lax.rem(y + offset, 8)
-        if phase == 1:
-            return zl * 8 + lax.rem(xc + offset, 8), t
-        other = lax.rem(z + offset, 8)
-        return lax.rem(other, 4) * 8 + xc, lax.div(other, 4) * 8 + y
-
-    place = (y, xc, z)
+            other = lax.rem(place[0] + offset, 16)
+            return s - core + lax.rem(other, 2), zh * 8 + lax.div(other, 2)
+        other = lax.rem(place[1] + offset, 32)
+        oz = lax.div(other, 4)
+        return (lax.rem(oz, 4) * 4 + lax.rem(other, 4)) * 2 + core, lax.div(oz, 4) * 8 + y
+
+    place = (y * 2 + core, z * 4 + x)
     has_lower, has_upper = s > 0, s < sectors - 1
 
+    own = [
+        pltpu.make_async_copy(wave_hbm.at[0], f.at[zh], load_sem.at[2]),
+        pltpu.make_async_copy(diag_hbm.at[0], dg.at[zh], load_sem.at[3]),
+    ]
     loads = [
         pltpu.make_async_copy(left_hbm, left, load_sem.at[0]),
         pltpu.make_async_copy(right_hbm, right, load_sem.at[1]),
     ]
-    for load in loads:
+    for load in own + loads:
         load.start()
 
     barrier = pltpu.get_barrier_semaphore()
@@ -104,11 +112,21 @@
             device_id_type=pl.DeviceIdType.MESH,
         )
 
-    for phase in range(3):
-        for offset in range(1, 8):
+    for phase in range(2):
+
+        def greet_peer(offset, carry, phase=phase):
             greet(*peer(phase, offset))
-    far_lower = jnp.logical_and(xc == 0, has_lower)
-    far_upper = jnp.logical_and(xc == 7, has_upper)
+            return carry
+
+        lax.fori_loop(1, SLOTS[phase], greet_peer, 0)
+    zt = (1 - zh) * 8 + y
+    ring_to = (zh * 8 + wrapped(y + 1, 8), zh * 8 + wrapped(y - 1, 8))
+    skip_to = (zh * 8 + wrapped(y + 2, 8), zh * 8 + wrapped(y - 2, 8))
+    cross_to = ((1 - zh) * 8 + wrapped(y + 1, 8), (1 - zh) * 8 + wrapped(y - 1, 8))
+    for term in cross_to:
+        greet(s, term)
+    far_lower = jnp.logical_and(core == 0, has_lower)
+    far_upper = jnp.logical_and(core == 1, has_upper)
 
     @pl.when(far_lower)
     def _():
@@ -117,10 +135,6 @@
     @pl.when(far_upper)
     def _():
         greet(s + 1, t)
-
-    f[zh] = wave[0]
-    dg[zh] = diag[0]
-    blocks[0, 1, zh, y] = wave[0].astype(BF16)
 
     @pl.when(s == 0)
     def _():
@@ -132,19 +146,17 @@
         for k in range(STEPS):
             blocks[k, 0] = jnp.zeros(blocks.shape[2:], BF16)
 
-    first_square = lane_sums(jnp.square(wave[0]))
-    pl.semaphore_wait(barrier, 21 + far_lower.astype(jnp.int32) + far_upper.astype(jnp.int32))
-
-    zt = (1 - zh) * 8 + y
-    ring_to = (zh * 8 + wrapped(y + 1, 8), zh * 8 + wrapped(y - 1, 8))
+    for load in own:
+        load.wait()
+    blocks[0, 1, zh, y] = f[zh].astype(BF16)
+    first_square = lane_sums(jnp.square(f[zh]))
+    pl.semaphore_wait(barrier, 48 + far_lower.astype(jnp.int32) + far_upper.astype(jnp.int32))
+
     first = [
         remote(blocks.at[0, 1, zh, y], blocks.at[0, 1, zh, y], first_send.at[0], first_recv.at[0], s, zt),
-        remote(wave.at[0], f.at[zh], first_send.at[1], first_recv.at[1], s, zt),
-        remote(diag.at[0], dg.at[zh], first_send.at[2], first_recv.at[2], s, zt),
+        remote(f.at[zh], f.at[zh], first_send.at[1], first_recv.at[1], s, zt),
+        remote(dg.at[zh], dg.at[zh], first_send.at[2], first_recv.at[2], s, zt),
     ]
-    for copy in first:
-        copy.start()
-    first[0].wait_recv()
 
     def position(d, distance):
         return wrapped(y - distance if d == 0 else y + distance, 8)
@@ -169,19 +181,51 @@
         def wait_piece(d, h, r):
             ring_copy(d, h, r).wait_recv()
 
-        for r in range(4):
-            for d, h in LONG:
-                if r:
-                    wait_piece(d, h, r - 1)
-                ring_copy(d, h, r).start()
-            for d, h in SHORT:
-                if r:
-                    wait_piece(d, h, r - 1)
-                if r < 3:
-                    ring_copy(d, h, r).start()
-            hand_on(k, lambda ref: ref.at[:, position(0, r)])
-            if r:
-                hand_on(k, lambda ref: ref.at[:, position(1, r)])
+        def start_skip(d, h):
+            piece = blocks.at[k, 1, h, position(d, 2)]
+            remote(piece, piece, ag_send.at[0], ag_recv.at[k, d, h, 3], s, skip_to[d]).start()
+
+        @pl.when(k == 0)
+        def _():
+            piece = blocks.at[0, 1, zh, y]
+            for d in range(2):
+                remote(piece, piece, ag_send.at[0], ag_recv.at[0, d, zh, 0], s, cross_to[d]).start()
+            first[0].start()
+            for d in range(2):
+                remote(piece, piece, ag_send.at[0], ag_recv.at[0, d, zh, 0], s, ring_to[d]).start()
+            for copy in first[1:]:
+                copy.start()
+
+        @pl.when(k > 0)
+        def _():
+            for d, h in LONG + SHORT:
+                ring_copy(d, h, 0).start()
+            hand_on(k, lambda ref: ref.at[:, y])
+
+        for d, h in LONG + SHORT:
+            wait_piece(d, h, 0)
+            ring_copy(d, h, 1).start()
+
+        @pl.when(k == 0)
+        def _():
+            first[0].wait_recv()
+            hand_on(k, lambda ref: ref.at[:, y])
+
+        for d in range(2):
+            hand_on(k, lambda ref: ref.at[:, position(d, 1)])
+        for d, h in LONG:
+            wait_piece(d, h, 1)
+            start_skip(d, h)
+            ring_copy(d, h, 2).start()
+        for d, h in SHORT:
+            wait_piece(d, h, 1)
+            ring_copy(d, h, 2).start()
+        for d in range(2):
+            hand_on(k, lambda ref: ref.at[:, position(d, 2)])
+        for d in range(2):
+            for h in range(2):
+                wait_piece(d, h, 2)
+            hand_on(k, lambda ref: ref.at[:, position(d, 3)])
         for d, h in LONG:
             wait_piece(d, h, 3)
         hand_on(k, lambda ref: ref.at[:, position(0, 4)])
@@ -210,11 +254,13 @@
         return lane_sums(total * mine.astype(F32))
 
     def pass_on(k, d, h, q):
-        where = destination(d, q)
-        value = image[h, where]
-        if q < (4 if (d, h) in LONG else 3):
-            rs_copy(k, d, h, q + 1).wait_recv()
-            value = value + rs_in[k, d, h, q].astype(F32)
+        value = image[h, destination(d, q)]
+        if q == 2:
+            rs_copy(k, d, h, 3).wait_recv()
+            value = value + rs_in[k, d, h, 2].astype(F32)
+            if (d, h) in LONG:
+                rs_copy(k, d, h, 4).wait_recv()
+                value = value + rs_in[k, d, h, 3].astype(F32)
         rs_out[k, d, h, q - 1] = value.astype(BF16)
         rs_copy(k, d, h, q).start()
 
@@ -225,27 +271,35 @@
             rs_send.at[0],
             rs_recv.at[k, d, h, q - 1],
             s,
-            ring_to[d],
+            skip_to[d] if q % 2 == 0 else ring_to[d],
         )
 
     def sum_start(k, phase, values):
+        sums = sc_in[phase]
         sc_out[k, phase] = values
-        sc_in[k, phase, place[phase]] = values
-        for offset in range(1, 8):
+        sums[k, place[phase]] = values
+
+        def send(offset, carry):
             remote(
                 sc_out.at[k, phase],
-                sc_in.at[k, phase, place[phase]],
+                sums.at[k, place[phase]],
                 sc_send.at[0],
                 sc_recv.at[k, phase],
                 *peer(phase, offset),
             ).start()
+            return carry
+
+        lax.fori_loop(1, SLOTS[phase], send, 0)
 
     def sum_end(k, phase):
-        arrived(sc_in.at[k, phase, pl.ds(0, 7)], sc_recv.at[k, phase])
-        return jnp.sum(sc_in[k, phase], axis=0)
+        sums = sc_in[phase]
+        arrived(sums.at[k, pl.ds(0, SLOTS[phase] - 1)], sc_recv.at[k, phase])
+        return jnp.sum(sums[k], axis=0)
 
     def pair(cross, square):
-        return jnp.concatenate([cross, square], axis=0)
+        lane = lax.broadcasted_iota(jnp.int32, (1, 128), 1)
+        cross, square = (jnp.sum(v, axis=1, keepdims=True) for v in (cross, square))
+        return jnp.where(lane < 64, cross, square)
 
     def step(k, square):
         gather(k)
@@ -258,36 +312,39 @@
         cross = apply_rows(k, (destination(0, 4), destination(0, 3)))
         for d, h in LONG:
             pass_on(k, d, h, 4)
-        pass_on(k, 0, 1, 3)
+        for h in range(2):
+            pass_on(k, 0, h, 3)
         cross += apply_rows(k, (destination(1, 3), destination(0, 2)))
-        pass_on(k, 1, 0, 3)
+        for h in range(2):
+            pass_on(k, 1, h, 3)
         cross += apply_rows(k, (destination(1, 2), destination(0, 1)))
-        for d, h in LONG:
-            pass_on(k, d, h, 3)
+        for h in range(2):
+            pass_on(k, 0, h, 1)
         cross += apply_rows(k, (destination(1, 1), y))
+        for h in range(2):
+            pass_on(k, 1, h, 1)
         sum_start(k, 0, pair(cross, square))
         for d, h in SHORT + LONG:
             pass_on(k, d, h, 2)
         sum_start(k, 1, sum_end(k, 0))
-        for d, h in SHORT + LONG:
-            pass_on(k, d, h, 1)
         for h in range(2):
+            total = image[h, y]
             for d in range(2):
-                rs_copy(k, d, h, 1).wait_recv()
-            z_out[k, h] = (image[h, y] + rs_in[k, 0, h, 0].astype(F32) + rs_in[k, 1, h, 0].astype(F32)).astype(BF16)
+                for q in (1, 2):
+                    rs_copy(k, d, h, q).wait_recv()
+                    total = total + rs_in[k, d, h, q - 1].astype(F32)
+            z_out[k, h] = total.astype(BF16)
         across = remote(z_out.at[k], z_in.at[k], z_send.at[0], z_recv.at[k], s, zt)
         across.start()
-        sum_start(k, 2, sum_end(k, 1))
-        sums = sum_end(k, 2)
-        both = jnp.sum(sums, axis=1, keepdims=True)
-        cross_total, square_total = both[0:1], both[1:2]
+        sums = sum_end(k, 1)
+        cross_total, square_total = sums[:, 0:1], sums[:, 64:65]
         theta = (cross_total / square_total)[None]
         scale = jnp.where(k == 0, 1.0, 1.0 / jnp.sqrt(square_total / total_size + 1e-06))[None]
 
         @pl.when(k == 0)
         def _():
-            first[1].wait_recv()
-            first[2].wait_recv()
+            first[1].wait()
+            first[2].wait()
 
         across.wait_recv()
         hpsi = (z_out[k].astype(F32) + z_in[k].astype(F32)) * scale
@@ -303,20 +360,20 @@
 
     square = lax.fori_loop(0, STEPS, step, first_square)
     last = pair(square, square)
-    for phase in range(3):
+    for phase in range(2):
         sum_start(STEPS, phase, last)
         last = sum_end(STEPS, phase)
-    norm = jnp.sum(last, axis=1, keepdims=True)[1:2]
+    norm = last[:, 64:65]
     out[0] = f[zh] / jnp.sqrt(norm / total_size + 1e-06)
 
-    for copy in first:
-        copy.wait_send()
+    first[0].wait_send()
     arrived(rs_in.at[:, :, :, pl.ds(0, 3)], ag_send.at[0])
     arrived(rs_in.at[:, 0, :, pl.ds(0, 1)], ag_send.at[0])
     arrived(rs_in.at[:, :, :, pl.ds(0, 3)], rs_send.at[0])
     arrived(rs_in.at[:, 0, :, pl.ds(0, 1)], rs_send.at[0])
     arrived(z_in, z_send.at[0])
-    arrived(sc_in.at[:, :, pl.ds(0, 7)], sc_send.at[0])
+    for phase in range(2):
+        arrived(sc_in[phase].at[:, pl.ds(0, SLOTS[phase] - 1)], sc_send.at[0])
 
     @pl.when(has_upper)
     def _():
@@ -335,7 +392,7 @@
     return pl.pallas_call(
         functools.partial(kernel, total_size),
         out_shape=jax.ShapeDtypeStruct(wave.shape, F32),
-        in_specs=[pl.BlockSpec(memory_space=pltpu.SMEM), vmem, vmem, hbm, hbm],
+        in_specs=[pl.BlockSpec(memory_space=pltpu.SMEM), hbm, hbm, hbm, hbm],
         out_specs=vmem,
         scratch_shapes=[
             pltpu.VMEM((4, 2, 8, ROWS, 512), BF16),
@@ -348,9 +405,10 @@
             pltpu.VMEM((STEPS, 2, ROWS, 512), BF16),
             pltpu.VMEM((2, ROWS, 512), F32),
             pltpu.VMEM((2, ROWS, 512), F32),
-            pltpu.VMEM((STEPS + 1, 3, 2, 128), F32),
-            pltpu.VMEM((STEPS + 1, 3, 8, 2, 128), F32),
-            dma((2,)),
+            pltpu.VMEM((STEPS + 1, 2, 1, 128), F32),
+            pltpu.VMEM((STEPS + 1, SLOTS[0], 1, 128), F32),
+            pltpu.VMEM((STEPS + 1, SLOTS[1], 1, 128), F32),
+            dma((4,)),
             dma((3,)),
             dma((3,)),
             dma((1,)),
@@ -362,10 +420,10 @@
             dma((1,)),
             dma((STEPS,)),
             dma((1,)),
-            dma((STEPS + 1, 3)),
+            dma((STEPS + 1, 2)),
         ],
         compiler_params=pltpu.CompilerParams(
-            collective_id=0, has_side_effects=True, vmem_limit_bytes=48 * 1024 * 1024
+            collective_id=0, has_side_effects=True, vmem_limit_bytes=67043328
         ),
         name="sweep",
     )(

time: 147 us -> 133 us (0.905)
  Pallas kernels: 140 us -> 132 us
  local copies, waits for them, and re-layouts: 6.15 us -> 1.47 us
    pallas_call x1, Pallas kernels: 140 us -> 132 us  [per_device(): pl.pallas_call(functools.partial(kernel, total_size), out_shape=jax.Shape...]
    unnamed x11 -> x1, local copies, waits for them, and re-layouts: 6.15 us -> 1.47 us
where the time goes in v2:
time: 133 us
  Pallas kernels  132 us (99%)
  local copies, waits for them, and re-layouts  1.47 us (1%)
    pallas_call x1, Pallas kernels, per_device(): pl.pallas_call(functools.partial(kernel, total_size), out_shape=jax.Shape...  132 us

profile of v2, /device:TPU:1, one launch (start us, length us, event | category | flops | bytes accessed | tf_op | source)
XLA Modules:
  0.0 133.2 jit_solution(11244031451989948618)
XLA Ops:
  0.0 131.7 %sweep.1 = f32[1,32,512]{2,1,0:T(8,128)} custom-call(s32[64]{0:T(128)} %charges.1, f32[1,32,512]{2,1,0:T(8,128)} %wave_hbm.1, f32[1,32,512]{2,1,0:T(8,128)} %diag_hbm.1, bf16[4,2,8,32,512]{4,3,2,1,0:T(8,128)(2,1)} %bitcast.2, bf16[4,512,512]{2,1,0:T(8,128)(2,1)} %bitcast.3), custom_call_target="tpu_custom_call" | custom-call | tf_op jit(solution)/shard_map/sweep/pallas_call | solution.py:392
  131.8 1.5 %copy.7 = f32[1,32,512]{2,1,0:T(8,128)} copy(f32[1,32,512]{2,1,0:T(8,128)} %sweep.1) | data formatting | bytes 131072

commit v3 on v2

--- a/solution.py
+++ b/solution.py
@@ -9,6 +9,16 @@
 
 STEPS = 3
 SLOTS = (16, 32)
+
+
+def hops(offset, count):
+    return min(offset % count, -offset % count)
+
+
+ORDER = (
+    sorted(range(1, 16), key=lambda o: -hops((o + 1) // 2, 8)),
+    sorted(range(1, 32), key=lambda o: -hops(o // 4, 8) - hops(o, 4)),
+)
 ROWS = 32
 BF16, F32 = jnp.bfloat16, jnp.float32
 LONG = ((0, 0), (1, 1))
@@ -279,7 +289,7 @@
         sc_out[k, phase] = values
         sums[k, place[phase]] = values
 
-        def send(offset, carry):
+        for offset in ORDER[phase]:
             remote(
                 sc_out.at[k, phase],
                 sums.at[k, place[phase]],
@@ -287,9 +297,6 @@
                 sc_recv.at[k, phase],
                 *peer(phase, offset),
             ).start()
-            return carry
-
-        lax.fori_loop(1, SLOTS[phase], send, 0)
 
     def sum_end(k, phase):
         sums = sc_in[phase]
@@ -309,23 +316,19 @@
             for load in loads:
                 load.wait()
 
-        cross = apply_rows(k, (destination(0, 4), destination(0, 3)))
+        cross = apply_rows(k, (destination(0, 4), destination(0, 3), destination(1, 3), destination(0, 2)))
         for d, h in LONG:
             pass_on(k, d, h, 4)
-        for h in range(2):
-            pass_on(k, 0, h, 3)
-        cross += apply_rows(k, (destination(1, 3), destination(0, 2)))
-        for h in range(2):
-            pass_on(k, 1, h, 3)
-        cross += apply_rows(k, (destination(1, 2), destination(0, 1)))
-        for h in range(2):
-            pass_on(k, 0, h, 1)
-        cross += apply_rows(k, (destination(1, 1), y))
-        for h in range(2):
-            pass_on(k, 1, h, 1)
+        for d in range(2):
+            for h in range(2):
+                pass_on(k, d, h, 3)
+        cross += apply_rows(k, (destination(1, 2), destination(0, 1), destination(1, 1), y))
         sum_start(k, 0, pair(cross, square))
         for d, h in SHORT + LONG:
             pass_on(k, d, h, 2)
+        for d in range(2):
+            for h in range(2):
+                pass_on(k, d, h, 1)
         sum_start(k, 1, sum_end(k, 0))
         for h in range(2):
             total = image[h, y]

time: 133 us -> 130 us (0.977)
  Pallas kernels: 132 us -> 129 us
    pallas_call x1, Pallas kernels: 132 us -> 129 us  [per_device(): pl.pallas_call(functools.partial(kernel, total_size), out_shape=jax.Shape...]
where the time goes in v3:
time: 130 us
  Pallas kernels  129 us (99%)
  local copies, waits for them, and re-layouts  1.47 us (1%)
    pallas_call x1, Pallas kernels, per_device(): pl.pallas_call(functools.partial(kernel, total_size), out_shape=jax.Shape...  129 us

profile of v3, /device:TPU:1, one launch (start us, length us, event | category | flops | bytes accessed | tf_op | source)
XLA Modules:
  0.0 130.2 jit_solution(14038685116229127463)
XLA Ops:
  0.0 128.7 %sweep.1 = f32[1,32,512]{2,1,0:T(8,128)} custom-call(s32[64]{0:T(128)} %charges.1, f32[1,32,512]{2,1,0:T(8,128)} %wave_hbm.1, f32[1,32,512]{2,1,0:T(8,128)} %diag_hbm.1, bf16[4,2,8,32,512]{4,3,2,1,0:T(8,128)(2,1)} %bitcast.2, bf16[4,512,512]{2,1,0:T(8,128)(2,1)} %bitcast.3), custom_call_target="tpu_custom_call" | custom-call | tf_op jit(solution)/shard_map/sweep/pallas_call | solution.py:395
  128.7 1.5 %copy.7 = f32[1,32,512]{2,1,0:T(8,128)} copy(f32[1,32,512]{2,1,0:T(8,128)} %sweep.1) | data formatting | bytes 131072

commit v4 on v3

--- a/solution.py
+++ b/solution.py
@@ -122,13 +122,9 @@
             device_id_type=pl.DeviceIdType.MESH,
         )
 
-    for phase in range(2):
-
-        def greet_peer(offset, carry, phase=phase):
+    for phase in (1, 0):
+        for offset in ORDER[phase]:
             greet(*peer(phase, offset))
-            return carry
-
-        lax.fori_loop(1, SLOTS[phase], greet_peer, 0)
     zt = (1 - zh) * 8 + y
     ring_to = (zh * 8 + wrapped(y + 1, 8), zh * 8 + wrapped(y - 1, 8))
     skip_to = (zh * 8 + wrapped(y + 2, 8), zh * 8 + wrapped(y - 2, 8))
@@ -324,11 +320,11 @@
                 pass_on(k, d, h, 3)
         cross += apply_rows(k, (destination(1, 2), destination(0, 1), destination(1, 1), y))
         sum_start(k, 0, pair(cross, square))
-        for d, h in SHORT + LONG:
-            pass_on(k, d, h, 2)
         for d in range(2):
             for h in range(2):
                 pass_on(k, d, h, 1)
+        for d, h in SHORT + LONG:
+            pass_on(k, d, h, 2)
         sum_start(k, 1, sum_end(k, 0))
         for h in range(2):
             total = image[h, y]

time: 130 us -> 128 us (0.985)
  Pallas kernels: 129 us -> 127 us
    pallas_call x1, Pallas kernels: 129 us -> 127 us  [per_device(): pl.pallas_call(functools.partial(kernel, total_size), out_shape=jax.Shape...]
where the time goes in v4:
time: 128 us
  Pallas kernels  127 us (99%)
  local copies, waits for them, and re-layouts  1.47 us (1%)
    pallas_call x1, Pallas kernels, per_device(): pl.pallas_call(functools.partial(kernel, total_size), out_shape=jax.Shape...  127 us

profile of v4, /device:TPU:1, one launch (start us, length us, event | category | flops | bytes accessed | tf_op | source)
XLA Modules:
  0.0 128.2 jit_solution(18196548768762279669)
XLA Ops:
  0.0 126.7 %sweep.1 = f32[1,32,512]{2,1,0:T(8,128)} custom-call(s32[64]{0:T(128)} %charges.1, f32[1,32,512]{2,1,0:T(8,128)} %wave_hbm.1, f32[1,32,512]{2,1,0:T(8,128)} %diag_hbm.1, bf16[4,2,8,32,512]{4,3,2,1,0:T(8,128)(2,1)} %bitcast.2, bf16[4,512,512]{2,1,0:T(8,128)(2,1)} %bitcast.3), custom_call_target="tpu_custom_call" | custom-call | tf_op jit(solution)/shard_map/sweep/pallas_call | solution.py:391
  126.7 1.5 %copy.7 = f32[1,32,512]{2,1,0:T(8,128)} copy(f32[1,32,512]{2,1,0:T(8,128)} %sweep.1) | data formatting | bytes 131072
